TPU v7x, 128 devices: a whole 4x4x4 slice. The times are simulated.
128 devices in a mesh: half: 4 (over y_hi, core), blk: 32 (over z, y_lo, x).
Axes of the slice: x: 4, y: 4 (y_hi: 2, y_lo: 2; y = y_hi * 2 + y_lo), z: 4, core: 2. Of those that a mesh axis runs over, the one named last changes fastest.
Arguments:
- sketch: float32 [131072, 256], P(('half', 'blk')), may hold values from -6 to 6
- near_field: float32 [131072, 64], P(('half', 'blk')), may hold values from -0.75 to 0.75
- source_one: float32 [131072, 128], P(('half', 'blk')), may hold values from -1 to 1
- source_two: float32 [131072, 128], P(('half', 'blk')), may hold values from -1 to 1
- target_one: float32 [131072, 128], P(('half', 'blk')), may hold values from -0.5 to 0.5
- target_two: float32 [131072, 128], P(('half', 'blk')), may hold values from -0.5 to 0.5
- quarter_mix: float32 [4096, 2, 128, 128], P(('half', 'blk')), may hold values from -0.375 to 0.375
- leaf_mix: float32 [4096, 2, 128, 128], P(('half', 'blk')), may hold values from -0.375 to 0.375
- target_mix_one: float32 [4096, 2, 128, 128], P(('half', 'blk')), may hold values from -0.375 to 0.375
- target_mix_two: float32 [4096, 2, 128, 128], P(('half', 'blk')), may hold values from -0.375 to 0.375
Outputs:
- product: float32 [131072, 256], P(('half', 'blk'))
All inputs are finite; a program needn't handle non-finite values.
Results may differ from a plain program's by a relative error of at most 0.000061.
Values sent between devices are 32-bit elements; how exact they have to be, the bound alone decides.
A program may use at most 128 MiB of HBM per device.

v0:
```python
import jax
import jax.numpy as jnp
from jax import lax
from jax.sharding import PartitionSpec as P

highest = lax.Precision.HIGHEST


def swapped(block, axis, apart):
    count = lax.axis_size(axis)
    route = []
    for low in range(count):
        high = low | 1 << apart
        if high != low and high < count:
            route += [(low, high), (high, low)]
    return lax.ppermute(block, axis, route)


def apply_nodes(matrices, coefficients):
    return jnp.einsum("nst,ntv->nsv", matrices, coefficients, precision=highest)


def apply_back(matrices, coefficients):
    return jnp.einsum("nts,ntv->nsv", matrices, coefficients, precision=highest)


def flip_pairs(coefficients):
    shaped = coefficients.reshape((coefficients.shape[0] // 2, 2) + coefficients.shape[1:])
    return shaped[:, ::-1].reshape(coefficients.shape)


def compress(basis, operand, groups):
    leaves = basis.reshape(groups, -1, basis.shape[1])
    blocks = operand.reshape(groups, -1, operand.shape[1])
    return jnp.einsum("nir,niv->nrv", leaves, blocks, precision=highest)


def expand(basis, coefficients, groups):
    leaves = basis.reshape(groups, -1, basis.shape[1])
    result = jnp.einsum("nir,nrv->niv", leaves, coefficients, precision=highest)
    return result.reshape(basis.shape[0], coefficients.shape[2])


def pair_quarter(coefficients):
    return swapped(coefficients, "half", 0)


def far_swap(coefficients):
    return swapped(coefficients, "half", 1)


def near_swap(coefficients):
    return swapped(coefficients, "half", 0)


def spread(coefficients):
    return lax.all_to_all(coefficients, "blk", split_axis=0, concat_axis=0, tiled=True)


def carry_nodes(first_load, second):
    result = (spread(far_swap(first_load)), spread(near_swap(second)))
    return result


def body(
    sketch,
    near_field,
    source_one,
    source_two,
    target_one,
    target_two,
    quarter_mix,
    leaf_mix,
    target_mix_one,
    target_mix_two,
):
    groups = lax.axis_size("blk")
    box_rows = near_field.shape[1]

    def apply_near(operand, pattern):
        near_boxes = near_field.reshape(groups // 2, box_rows, box_rows)
        blocks = operand.reshape(groups // 2, box_rows, operand.shape[1])
        return jnp.einsum(pattern, near_boxes, blocks, precision=highest).reshape(operand.shape)

    coef_one = compress(source_one, sketch, groups)
    mixed_one = apply_nodes(quarter_mix[:, 0], coef_one) + apply_nodes(
        quarter_mix[:, 1], pair_quarter(coef_one)
    )
    coef_two = compress(source_two, sketch, groups)
    mixed_two = apply_nodes(leaf_mix[:, 0], coef_two) + apply_nodes(
        leaf_mix[:, 1], flip_pairs(coef_two)
    )
    arrived_one, arrived_two = carry_nodes(mixed_one, mixed_two)
    out_one = apply_nodes(target_mix_one[:, 0], arrived_one) + apply_nodes(
        target_mix_one[:, 1], flip_pairs(arrived_one)
    )
    out_two = apply_nodes(target_mix_two[:, 0], arrived_two) + apply_nodes(
        target_mix_two[:, 1], flip_pairs(arrived_two)
    )
    operand = (
        0.5 * sketch
        + apply_near(sketch, "kij,kjv->kiv")
        + expand(target_one, out_one, groups)
        + expand(target_two, out_two, groups)
    )
    head_one = compress(target_one, operand, groups)
    back_one = apply_back(target_mix_one[:, 0], head_one) + flip_pairs(
        apply_back(target_mix_one[:, 1], head_one)
    )
    head_two = compress(target_two, operand, groups)
    back_two = apply_back(target_mix_two[:, 0], head_two) + flip_pairs(
        apply_back(target_mix_two[:, 1], head_two)
    )
    landed_one, landed_two = carry_nodes(back_one, back_two)
    tail_one = apply_back(quarter_mix[:, 0], landed_one) + pair_quarter(
        apply_back(quarter_mix[:, 1], landed_one)
    )
    tail_two = apply_back(leaf_mix[:, 0], landed_two) + flip_pairs(
        apply_back(leaf_mix[:, 1], landed_two)
    )
    return (
        0.5 * operand
        + apply_near(operand, "kji,kjv->kiv")
        + expand(source_one, tail_one, groups)
        + expand(source_two, tail_two, groups)
    )


def solution(mesh):
    placed = (
        P(("half", "blk"), None),
        P(("half", "blk"), None),
        P(("half", "blk"), None),
        P(("half", "blk"), None),
        P(("half", "blk"), None),
        P(("half", "blk"), None),
        P(("half", "blk"), None, None, None),
        P(("half", "blk"), None, None, None),
        P(("half", "blk"), None, None, None),
        P(("half", "blk"), None, None, None),
    )
    return jax.shard_map(
        body, mesh=mesh, in_specs=placed, out_specs=P(("half", "blk"), None), check_vma=False
    )
```

profile of v0, /device:TPU:1, one launch (start us, length us, event | category | flops | bytes accessed | tf_op | source)
XLA Modules:
  0.0 562.0 jit_solution(12752151659820376219)
XLA Ops:
  0.0 7.0 %fusion.51 = f32[32,128,256]{2,1,0:T(8,128)} fusion(f32[32,32,128]{2,1,0:T(8,128)} %bitcast.182, f32[32,32,256]{2,1,0:T(8,128)} %bitcast.177), kind=kOutput, calls=%fused_computation.64 | convolution fusion | flops 402653184 | bytes 5767168 | tf_op jit(solution)/shard_map/nir,niv->nrv/dot_general | solution.py:35
  7.0 1.5 collective-permute-start
  8.5 0.0 copy-done.12
  8.5 3.6 fusion.52
  12.1 0.0 copy-done.9
  12.1 0.0 copy-start.5
  12.1 8.9 %fusion.16 = f32[32,256,128]{2,1,0:T(8,128)} fusion(f32[32,128,256]{2,1,0:T(8,128)S(1)} %fusion.52, f32[32,2,128,128]{3,2,1,0:T(8,128)S(1)} %copy-done.9), kind=kOutput, calls=%fused_computation.23 | convolution fusion | flops 1610612736 | bytes 10485760 | tf_op jit(solution)/shard_map/nst,ntv->nsv/dot_general | solution.py:20
  21.1 0.0 copy-done.5
  21.1 4.6 rev.19
  25.7 10.0 %add_bitcast_fusion = f32[32,128,256]{1,2,0:T(8,128)S(1)} fusion(f32[32,256,128]{2,1,0:T(8,128)} %fusion.16, f32[32,128,256]{2,1,0:T(8,128)} %bitcast.171, f32[32,2,128,128]{3,2,1,0:T(8,128)} %param.17), kind=kOutput, calls=%fused_computation.7 | convolution fusion | flops 1611661312 | bytes 14680064 | tf_op jit(solution)/shard_map/nst,ntv->nsv/dot_general | solution.py:20
  35.7 0.3 collective-permute-start.2
  36.0 9.1 %fusion.29 = f32[32,256,128]{2,1,0:T(8,128)S(1)} fusion(f32[32,128,256]{2,1,0:T(8,128)} %fusion.51, f32[32,2,128,128]{3,2,1,0:T(8,128)S(1)} %copy-done.10), kind=kOutput, calls=%fused_computation.36 | convolution fusion | flops 1610612736 | bytes 10485760 | tf_op jit(solution)/shard_map/nst,ntv->nsv/dot_general | solution.py:20
  45.2 0.0 collective-permute-done
  45.2 9.1 %add_bitcast_fusion.1 = f32[32,128,256]{1,2,0:T(8,128)S(1)} fusion(f32[32,256,128]{2,1,0:T(8,128)S(1)} %fusion.29, f32[32,128,256]{2,1,0:T(8,128)} %collective-permute-done, f32[32,2,128,128]{3,2,1,0:T(8,128)S(1)} %copy-done.10), kind=kOutput, calls=%fused_computation.10 | convolution fusion | flops 1611661312 | bytes 14680064 | tf_op jit(solution)/shard_map/nst,ntv->nsv/dot_general | solution.py:20
  54.4 3.1 collective-permute-start.1
  57.5 0.0 collective-permute-done.2
  57.5 137.2 %all_to_all.20 = f32[32,128,256]{1,2,0:T(8,128)} all-to-all(f32[32,128,256]{1,2,0:T(8,128)S(1)} %collective-permute-done.2), channel_id=1, replica_groups=mesh['half'=4,'blk'=32] {'blk'}, dimensions={0} | all-to-all | bytes 8388608 | tf_op jit(solution)/shard_map/all_to_all | solution.py:57
  194.7 0.0 collective-permute-done.1
  194.7 8.3 %all-to-all-start = ((f32[32,128,256]{1,2,0:T(8,128)}), f32[32,128,256]{1,2,0:T(8,128)}, u32[]{:S(2)}, u32[]{:S(2)}) async-start(f32[32,128,256]{1,2,0:T(8,128)} %collective-permute-done.1), calls=%async_computation | async-start | bytes 8388608 | tf_op jit(solution)/shard_map/all_to_all | solution.py:57
  203.1 0.1 reshape.88
  203.2 2.1 fusion.47
  205.3 4.6 rev.20
  209.9 6.0 %fusion.7 = f32[32,256,128]{2,1,0:T(8,128)S(1)} fusion(f32[32,128,256]{1,2,0:T(8,128)} %bitcast.172, f32[32,2,128,128]{3,2,1,0:T(8,128)} %param.19), kind=kOutput, calls=%fused_computation.14 | convolution fusion | flops 1610612736 | bytes 10485760 | tf_op jit(solution)/shard_map/nst,ntv->nsv/dot_general | solution.py:20
  216.0 0.0 copy-start.15
  216.0 4.6 fusion.10
  220.6 5.2 fusion.1
  225.8 30.2 %all-to-all-done = f32[32,128,256]{1,2,0:T(8,128)} async-done(((f32[32,128,256]{1,2,0:T(8,128)}), f32[32,128,256]{1,2,0:T(8,128)}, u32[]{:S(2)}, u32[]{:S(2)}) %all-to-all-start) | async-done | bytes 4194336 | tf_op jit(solution)/shard_map/all_to_all | solution.py:57
  255.9 4.7 rev.18
  260.6 6.2 %fusion.20 = f32[32,256,128]{2,1,0:T(8,128)S(1)} fusion(f32[32,128,256]{1,2,0:T(8,128)} %bitcast.173, f32[32,2,128,128]{3,2,1,0:T(8,128)} %param.18), kind=kOutput, calls=%fused_computation.27 | convolution fusion | flops 1610612736 | bytes 10485760 | tf_op jit(solution)/shard_map/nst,ntv->nsv/dot_general | solution.py:20
  266.8 5.7 %fusion.23 = f32[32,256,128]{2,1,0:T(8,128)S(1)} fusion(f32[32,128,256]{1,2,0:T(8,128)} %all-to-all-done, f32[32,2,128,128]{3,2,1,0:T(8,128)S(1)} %copy-done.6), kind=kOutput, calls=%fused_computation.30 | convolution fusion | flops 1610612736 | bytes 10485760 | tf_op jit(solution)/shard_map/nst,ntv->nsv/dot_general | solution.py:20
  272.6 0.0 copy-start.13
  272.6 4.2 fusion.3
  276.8 0.3 bitcast_add_fusion.8
  277.2 7.4 %fusion.53 = f32[32,256,128]{2,1,0:T(8,128)S(1)} fusion(f32[32,32,256]{2,1,0:T(8,128)S(1)} %bitcast.168, f32[32,32,128]{2,1,0:T(8,128)S(1)} %bitcast.165), kind=kOutput, calls=%fused_computation.66 | convolution fusion | flops 402653184 | bytes 5767168 | tf_op jit(solution)/shard_map/nir,niv->nrv/dot_general | solution.py:35
  284.6 5.8 %fusion.18 = f32[32,256,128]{2,1,0:T(8,128)} fusion(f32[32,256,128]{2,1,0:T(8,128)S(1)} %fusion.53, f32[32,2,128,128]{3,2,1,0:T(8,128)S(1)} %copy-done.6), kind=kOutput, calls=%fused_computation.25 | convolution fusion | flops 1610612736 | bytes 10485760 | tf_op jit(solution)/shard_map/nts,ntv->nsv/dot_general | solution.py:24
  290.4 4.6 rev.21
  295.0 8.7 %bitcast_add_fusion.4 = f32[32,128,256]{1,2,0:T(8,128)} fusion(f32[16,2,128,256]{2,3,1,0:T(8,128)} %rev.21, f32[32,256,128]{2,1,0:T(8,128)} %copy-done.2, f32[32,2,128,128]{3,2,1,0:T(8,128)} %param.18), kind=kOutput, calls=%fused_computation.4 | convolution fusion | flops 1611661312 | bytes 14680064 | tf_op jit(solution)/shard_map/nts,ntv->nsv/dot_general | solution.py:24
  303.7 0.5 collective-permute-start.3
  304.2 7.4 %fusion.54 = f32[32,256,128]{2,1,0:T(8,128)S(1)} fusion(f32[32,32,256]{2,1,0:T(8,128)S(1)} %bitcast.169, f32[32,32,128]{2,1,0:T(8,128)S(1)} %bitcast.181), kind=kOutput, calls=%fused_computation.67 | convolution fusion | flops 402653184 | bytes 5767168 | tf_op jit(solution)/shard_map/nir,niv->nrv/dot_general | solution.py:35
  311.6 5.5 fusion.5
  317.1 4.6 rev.22
  321.7 8.7 %bitcast_add_fusion.1 = f32[32,128,256]{1,2,0:T(8,128)} fusion(f32[16,2,128,256]{2,3,1,0:T(8,128)} %rev.22, f32[32,256,128]{2,1,0:T(8,128)} %copy-done.3, f32[32,2,128,128]{3,2,1,0:T(8,128)} %param.19), kind=kOutput, calls=%fused_computation.1 | convolution fusion | flops 1611661312 | bytes 14680064 | tf_op jit(solution)/shard_map/nts,ntv->nsv/dot_general | solution.py:24
  330.4 3.0 collective-permute-start.5
  333.4 61.7 %collective-permute-done.3 = f32[32,128,256]{1,2,0:T(8,128)} collective-permute-done((f32[32,128,256]{1,2,0:T(8,128)}, f32[32,128,256]{1,2,0:T(8,128)}, u32[]{:S(2)}, u32[]{:S(2)}) %collective-permute-start.3) | collective-permute-done | bytes 4194336 | tf_op jit(solution)/shard_map/ppermute | solution.py:16
  395.1 10.3 %all-to-all-start.2 = ((f32[32,128,256]{1,2,0:T(8,128)}), f32[32,128,256]{1,2,0:T(8,128)}, u32[]{:S(2)}, u32[]{:S(2)}) async-start(f32[32,128,256]{1,2,0:T(8,128)} %collective-permute-done.3), calls=%async_computation.2 | async-start | bytes 8388608 | tf_op jit(solution)/shard_map/all_to_all | solution.py:57
  405.4 0.0 collective-permute-done.5
  405.4 53.7 %all-to-all-done.2 = f32[32,128,256]{1,2,0:T(8,128)} async-done(((f32[32,128,256]{1,2,0:T(8,128)}), f32[32,128,256]{1,2,0:T(8,128)}, u32[]{:S(2)}, u32[]{:S(2)}) %all-to-all-start.2) | async-done | bytes 4194336 | tf_op jit(solution)/shard_map/all_to_all | solution.py:57
  459.1 7.8 %all-to-all-start.3 = ((f32[32,128,256]{1,2,0:T(8,128)}), f32[32,128,256]{1,2,0:T(8,128)}, u32[]{:S(2)}, u32[]{:S(2)}) async-start(f32[32,128,256]{1,2,0:T(8,128)} %collective-permute-done.5), calls=%async_computation.3 | async-start | bytes 8388608 | tf_op jit(solution)/shard_map/all_to_all | solution.py:57
  467.0 8.8 %convolution_bitcast_fusion = f32[32,128,256]{2,1,0:T(8,128)} fusion(f32[32,128,256]{1,2,0:T(8,128)} %all-to-all-done.2, f32[32,2,128,128]{3,2,1,0:T(8,128)} %param.16), kind=kOutput, calls=%fused_computation.11 | convolution fusion | flops 1610612736 | bytes 10485760 | tf_op jit(solution)/shard_map/nts,ntv->nsv/dot_general | solution.py:24
  475.8 2.5 collective-permute-start.4
  478.2 1.1 fusion.49
  479.4 40.6 %all-to-all-done.3 = f32[32,128,256]{1,2,0:T(8,128)} async-done(((f32[32,128,256]{1,2,0:T(8,128)}), f32[32,128,256]{1,2,0:T(8,128)}, u32[]{:S(2)}, u32[]{:S(2)}) %all-to-all-start.3) | async-done | bytes 4194336 | tf_op jit(solution)/shard_map/all_to_all | solution.py:57
  520.0 8.1 %fusion.12 = f32[32,256,128]{2,1,0:T(8,128)} fusion(f32[32,128,256]{1,2,0:T(8,128)} %all-to-all-done.3, f32[32,2,128,128]{3,2,1,0:T(8,128)} %param.17), kind=kOutput, calls=%fused_computation.19 | convolution fusion | flops 1610612736 | bytes 10485760 | tf_op jit(solution)/shard_map/nts,ntv->nsv/dot_general | solution.py:24
  528.1 4.6 rev.23
  532.7 5.4 copy.25
  538.1 8.8 %bitcast_add_fusion = f32[32,128,256]{2,1,0:T(8,128)S(1)} fusion(f32[16,2,128,256]{3,2,1,0:T(8,128)} %copy.25, f32[32,128,256]{1,2,0:T(8,128)} %all-to-all-done.3, f32[32,2,128,128]{3,2,1,0:T(8,128)} %param.17), kind=kOutput, calls=%fused_computation | convolution fusion | flops 1611661312 | bytes 14680064 | tf_op jit(solution)/shard_map/nts,ntv->nsv/dot_general | solution.py:24
  546.9 0.0 copy-start.11
  546.9 2.4 fusion.55
  549.3 0.0 copy-start.17
  549.3 6.2 %fusion.27 = f32[32,256,128]{1,2,0:T(8,128)S(1)} fusion(f32[32,128,256]{1,2,0:T(8,128)} %all-to-all-done.2, f32[32,2,128,128]{3,2,1,0:T(8,128)S(1)} %copy-done.11), kind=kOutput, calls=%fused_computation.34 | convolution fusion | flops 1610612736 | bytes 10485760 | tf_op jit(solution)/shard_map/nts,ntv->nsv/dot_general | solution.py:24
  555.6 0.0 collective-permute-done.4
  555.6 0.0 copy-start.1
  555.6 4.8 fusion
  560.4 1.3 bitcast_add_fusion.5
  (33 shorter events, 0.1 us)
Async XLA Ops:
  0.0 272.6 %copy-start = (f32[1024,128]{1,0:T(8,128)S(1)}, f32[1024,128]{1,0:T(8,128)}, u32[]{:S(2)}) copy-start(f32[1024,128]{1,0:T(8,128)} %param.14) | copy-start | bytes 1572868
  0.0 8.5 %copy-start.12 = (f32[1024,256]{1,0:T(8,128)S(1)}, f32[1024,256]{1,0:T(8,128)}, u32[]{:S(2)}) copy-start(f32[1024,256]{1,0:T(8,128)} %param.10) | copy-start | bytes 3145732
  0.0 8.5 %copy-start.18 = (f32[1024,128]{1,0:T(8,128)S(1)}, f32[1024,128]{1,0:T(8,128)}, u32[]{:S(2)}) copy-start(f32[1024,128]{1,0:T(8,128)} %param.13) | copy-start | bytes 1572868
  7.0 5.1 copy-start.9
  7.0 38.2 %collective-permute-start = (f32[32,128,256]{2,1,0:T(8,128)}, f32[32,128,256]{2,1,0:T(8,128)}, u32[]{:S(2)}, u32[]{:S(2)}) collective-permute-start(f32[32,128,256]{2,1,0:T(8,128)} %fusion.51), channel_id=1, source_target_pairs={{0,32},{32,0},{64,96},{96,64},{1,33},{33,1},{65,97},{97,65},{2,34}... | collective-permute-start | bytes 12582920 | tf_op jit(solution)/shard_map/ppermute | solution.py:16
  12.1 9.0 %copy-start.5 = (f32[32,128,256]{2,1,0:T(8,128)}, f32[32,128,256]{2,1,0:T(8,128)S(1)}, u32[]{:S(2)}) copy-start(f32[32,128,256]{2,1,0:T(8,128)S(1)} %fusion.52) | copy-start | bytes 12582916
  25.7 10.4 %copy-start.10 = (f32[32,2,128,128]{3,2,1,0:T(8,128)S(1)}, f32[32,2,128,128]{3,2,1,0:T(8,128)}, u32[]{:S(2)}) copy-start(f32[32,2,128,128]{3,2,1,0:T(8,128)} %param.16) | copy-start | bytes 12582916
  35.7 21.8 %collective-permute-start.2 = (f32[32,128,256]{1,2,0:T(8,128)S(1)}, f32[32,128,256]{1,2,0:T(8,128)S(1)}, u32[]{:S(2)}, u32[]{:S(2)}) collective-permute-start(f32[32,128,256]{1,2,0:T(8,128)S(1)} %add_bitcast_fusion), channel_id=1, source_target_pairs={{0,32},{32,0},{64,96},{96,64},{1,33},{33,1},{65,97},{97,65},{2,34}... | collective-permute-start | bytes 12582920 | tf_op jit(solution)/shard_map/ppermute | solution.py:16
  54.4 140.4 %collective-permute-start.1 = (f32[32,128,256]{1,2,0:T(8,128)S(1)}, f32[32,128,256]{1,2,0:T(8,128)}, u32[]{:S(2)}, u32[]{:S(2)}) collective-permute-start(f32[32,128,256]{1,2,0:T(8,128)S(1)} %add_bitcast_fusion.1), channel_id=1, source_target_pairs={{0,64},{64,0},{32,96},{96,32},{1,65},{65,1},{33,97},{97,33},{2,66}... | collective-permute-start | bytes 12582920 | tf_op jit(solution)/shard_map/ppermute | solution.py:16
  194.7 8.3 %copy-start.20 = (f32[1024,64]{0,1:T(8,128)S(1)}, f32[1024,64]{0,1:T(8,128)}, u32[]{:S(2)}) copy-start(f32[1024,64]{0,1:T(8,128)} %param.11) | copy-start | bytes 786436
  194.7 61.2 %all-to-all-start = ((f32[32,128,256]{1,2,0:T(8,128)}), f32[32,128,256]{1,2,0:T(8,128)}, u32[]{:S(2)}, u32[]{:S(2)}) async-start(f32[32,128,256]{1,2,0:T(8,128)} %collective-permute-done.1), calls=%async_computation | async-start | bytes 8388608 | tf_op jit(solution)/shard_map/all_to_all | solution.py:57
  209.9 6.0 %copy-start.4 = (f32[32,128,256]{1,2,0:T(8,128)S(1)}, f32[32,128,256]{1,2,0:T(8,128)}, u32[]{:S(2)}) copy-start(f32[32,128,256]{1,2,0:T(8,128)} %all_to_all.20) | copy-start | bytes 12582916
  209.9 6.0 %copy-start.7 = (f32[32,2,128,128]{3,2,1,0:T(8,128)S(1)}, f32[32,2,128,128]{3,2,1,0:T(8,128)}, u32[]{:S(2)}) copy-start(f32[32,2,128,128]{3,2,1,0:T(8,128)} %param.19) | copy-start | bytes 12582916
  216.0 4.6 copy-start.15
  260.6 6.2 %copy-start.6 = (f32[32,2,128,128]{3,2,1,0:T(8,128)S(1)}, f32[32,2,128,128]{3,2,1,0:T(8,128)}, u32[]{:S(2)}) copy-start(f32[32,2,128,128]{3,2,1,0:T(8,128)} %param.18) | copy-start | bytes 12582916
  272.6 4.2 copy-start.13
  272.6 4.2 copy-start.14
  284.6 5.8 %copy-start.2 = (f32[32,256,128]{2,1,0:T(8,128)}, f32[32,256,128]{2,1,0:T(8,128)S(1)}, u32[]{:S(2)}) copy-start(f32[32,256,128]{2,1,0:T(8,128)S(1)} %fusion.53) | copy-start | bytes 12582916
  295.0 9.1 %copy-start.16 = (f32[1024,128]{1,0:T(8,128)S(1)}, f32[1024,128]{1,0:T(8,128)}, u32[]{:S(2)}) copy-start(f32[1024,128]{1,0:T(8,128)} %param.15) | copy-start | bytes 1572868
  303.7 7.9 %copy-start.8 = (f32[32,2,128,128]{3,2,1,0:T(8,128)S(1)}, f32[32,2,128,128]{3,2,1,0:T(8,128)}, u32[]{:S(2)}) copy-start(f32[32,2,128,128]{3,2,1,0:T(8,128)} %param.19) | copy-start | bytes 12582916
  303.7 91.5 %collective-permute-start.3 = (f32[32,128,256]{1,2,0:T(8,128)}, f32[32,128,256]{1,2,0:T(8,128)}, u32[]{:S(2)}, u32[]{:S(2)}) collective-permute-start(f32[32,128,256]{1,2,0:T(8,128)} %bitcast_add_fusion.4), channel_id=1, source_target_pairs={{0,64},{64,0},{32,96},{96,32},{1,65},{65,1},{33,97},{97,33},{2,66}... | collective-permute-start | bytes 12582920 | tf_op jit(solution)/shard_map/ppermute | solution.py:16
  311.6 5.5 copy-start.3
  330.4 75.0 %collective-permute-start.5 = (f32[32,128,256]{1,2,0:T(8,128)}, f32[32,128,256]{1,2,0:T(8,128)}, u32[]{:S(2)}, u32[]{:S(2)}) collective-permute-start(f32[32,128,256]{1,2,0:T(8,128)} %bitcast_add_fusion.1), channel_id=1, source_target_pairs={{0,32},{32,0},{64,96},{96,64},{1,33},{33,1},{65,97},{97,65},{2,34}... | collective-permute-start | bytes 12582920 | tf_op jit(solution)/shard_map/ppermute | solution.py:16
  395.1 64.0 %all-to-all-start.2 = ((f32[32,128,256]{1,2,0:T(8,128)}), f32[32,128,256]{1,2,0:T(8,128)}, u32[]{:S(2)}, u32[]{:S(2)}) async-start(f32[32,128,256]{1,2,0:T(8,128)} %collective-permute-done.3), calls=%async_computation.2 | async-start | bytes 8388608 | tf_op jit(solution)/shard_map/all_to_all | solution.py:57
  459.1 60.8 %all-to-all-start.3 = ((f32[32,128,256]{1,2,0:T(8,128)}), f32[32,128,256]{1,2,0:T(8,128)}, u32[]{:S(2)}, u32[]{:S(2)}) async-start(f32[32,128,256]{1,2,0:T(8,128)} %collective-permute-done.5), calls=%async_computation.3 | async-start | bytes 8388608 | tf_op jit(solution)/shard_map/all_to_all | solution.py:57
  475.8 79.8 %collective-permute-start.4 = (f32[32,128,256]{2,1,0:T(8,128)}, f32[32,128,256]{2,1,0:T(8,128)}, u32[]{:S(2)}, u32[]{:S(2)}) collective-permute-start(f32[32,128,256]{2,1,0:T(8,128)} %convolution_bitcast_fusion), channel_id=1, source_target_pairs={{0,32},{32,0},{64,96},{96,64},{1,33},{33,1},{65,97},{97,65},{2,34}... | collective-permute-start | bytes 12582920 | tf_op jit(solution)/shard_map/ppermute | solution.py:16
  538.1 8.8 %copy-start.19 = (f32[1024,128]{1,0:T(8,128)S(1)}, f32[1024,128]{1,0:T(8,128)}, u32[]{:S(2)}) copy-start(f32[1024,128]{1,0:T(8,128)} %param.13) | copy-start | bytes 1572868
  546.9 2.4 copy-start.11
  549.3 6.3 %copy-start.17 = (f32[1024,128]{1,0:T(8,128)S(1)}, f32[1024,128]{1,0:T(8,128)}, u32[]{:S(2)}) copy-start(f32[1024,128]{1,0:T(8,128)} %param.12) | copy-start | bytes 1572868
  555.6 6.1 %copy-start.1 = (f32[1024,128]{1,0:T(8,128)S(1)}, f32[1024,128]{1,0:T(8,128)}, u32[]{:S(2)}) copy-start(f32[1024,128]{1,0:T(8,128)} %param.14) | copy-start | bytes 1572868
where the time goes:
time: 572 us; the launch traced here: 562 us
  waiting for transfers between devices  186 us (33%)
  matrix products  166 us (29%)
  blocking collectives  137 us (24%)
  starting transfers between devices  37.3 us (7%)
  local copies, waits for them, and re-layouts  33.4 us (6%)
    all_to_all x1, blocking collectives, spread(): lax.all_to_all(coefficients, 'blk', split_axis=0, concat_axis=0, tiled=True)  137 us
    all_to_all x3, waiting for transfers between devices, spread(): lax.all_to_all(coefficients, 'blk', split_axis=0, concat_axis=0, tiled=True)  125 us
    ppermute x6, waiting for transfers between devices, swapped(): return lax.ppermute(block, axis, route)  61.7 us
    dot_general x8, matrix products, apply_back(): return jnp.einsum('nts,ntv->nsv', matrices, coefficients, precision=highest)  60.5 us
    dot_general x8, matrix products, apply_nodes(): return jnp.einsum('nst,ntv->nsv', matrices, coefficients, precision=highest)  59.8 us
    rev x7, local copies, waits for them, and re-layouts, flip_pairs(): return shaped[:, ::-1].reshape(coefficients.shape)  33.1 us
    all_to_all x3, starting transfers between devices, spread(): lax.all_to_all(coefficients, 'blk', split_axis=0, concat_axis=0, tiled=True)  26.4 us
    dot_general x4, matrix products, compress(): return jnp.einsum('nir,niv->nrv', leaves, blocks, precision=highest)  25.4 us
  transfers between devices with their start and end apart: 9, of which 4 were waited for; matrix products, arithmetic and copies ran while one was open for 25% of the time, Pallas kernels for 0%

commit v1 on v0

v1 whole, which is shorter than its diff:
```python
import functools

import jax
import jax.numpy as jnp
from jax import lax
from jax.experimental import pallas as pl
from jax.experimental.pallas import tpu as pltpu
from jax.sharding import PartitionSpec as P

MESH = pl.DeviceIdType.MESH
HIGH = lax.Precision.HIGHEST
F32 = jnp.float32


def dot(a, b):
    return lax.dot_general(a, b, (((1,), (0,)), ((), ())), precision=HIGH, preferred_element_type=F32)


def dot_nt(a, b):
    return lax.dot_general(a, b, (((1,), (1,)), ((), ())), precision=HIGH, preferred_element_type=F32)


def dot_tn(a, b):
    return lax.dot_general(a, b, (((0,), (0,)), ((), ())), precision=HIGH, preferred_element_type=F32)


def xor(a, b, bits):
    total = 0
    for k in range(bits):
        w = 1 << k
        total = total + lax.rem(lax.div(a, w) + lax.div(b, w), 2) * w
    return total


def reversed_bits(a, bits):
    total = 0
    for k in range(bits):
        total = total + lax.rem(lax.div(a, 1 << k), 2) * (1 << (bits - 1 - k))
    return total


def rows(ref, start, count):
    return ref.at[pl.ds(pl.multiple_of(start, 32), count)]


def kernel(
    groups,
    sketch,
    near,
    source_one,
    source_two,
    target_one,
    target_two,
    quarter_mix,
    leaf_mix,
    target_mix_one,
    target_mix_two,
    product,
    v_own,
    near_own,
    s_one,
    s_one_peer,
    s_two,
    t_one,
    t_two,
    qm,
    lm,
    tm_one,
    tm_two,
    a_send,
    b_send,
    a_recv,
    b_recv,
    vf,
    vc,
    p_one,
    p_two,
    yf,
    yx,
    yc,
    yf_recv,
    yc_recv,
    load_sem,
    mix_sem,
    peer_sem,
    send_sem,
    vf_sem,
    vp_sem,
    vc_sem,
    a_sem,
    b_sem,
    x_sem,
    yf_sem,
    yc_sem,
):
    pairs = groups // 2
    bits = pairs.bit_length() - 1
    q = lax.axis_index("half")
    m = lax.axis_index("blk")
    mine = lax.div(m, 2)
    q_peer = xor(q, 1, 2)
    q_far = xor(q, 2, 2)

    def pair_at(step):
        return xor(mine, reversed_bits(step, bits), bits)

    barrier = pltpu.get_barrier_semaphore()

    def greet(n, carry):
        pl.semaphore_signal(barrier, inc=1, device_id=(q_far, n), device_id_type=MESH)
        pl.semaphore_signal(barrier, inc=1, device_id=(q_peer, n), device_id_type=MESH)
        return carry

    lax.fori_loop(0, groups, greet, 0)

    loads = [
        pltpu.make_async_copy(src, dst, load_sem.at[k])
        for k, (src, dst) in enumerate(
            (
                (sketch, v_own),
                (source_one, s_one),
                (source_two, s_two),
                (target_one, t_one),
                (target_two, t_two),
                (near, near_own),
            )
        )
    ]
    for copy in loads:
        copy.start()

    def mix_copy(k, p):
        src, dst = ((quarter_mix, qm), (leaf_mix, lm), (target_mix_one, tm_one), (target_mix_two, tm_two))[k]
        here = pl.ds(2 * p, 2)
        return pltpu.make_async_copy(src.at[here], dst.at[here], mix_sem.at[k, p])

    def load_source_mix(step, carry):
        p = pair_at(step)
        mix_copy(0, p).start()
        mix_copy(1, p).start()
        return carry

    def load_target_mix(step, carry):
        p = pair_at(step)
        mix_copy(2, p).start()
        mix_copy(3, p).start()
        return carry

    lax.fori_loop(0, pairs, load_source_mix, 0)
    lax.fori_loop(0, pairs, load_target_mix, 0)

    def remote(src, dst, k, recv, to):
        return pltpu.make_async_remote_copy(
            src_ref=src, dst_ref=dst, send_sem=send_sem.at[k], recv_sem=recv, device_id=to, device_id_type=MESH
        )

    def vf_copy(n):
        return remote(rows(v_own, 32 * n, 32), rows(vf, 64 * m, 32), 0, vf_sem.at[m], (q_far, n))

    def vc_copy(p, n):
        return remote(rows(v_own, 64 * p, 64), rows(vc, 64 * m, 64), 1, vc_sem.at[m], (q_peer, n))

    def a_copy(n):
        return remote(rows(a_send, 64 * n, 64), rows(a_recv, 64 * m, 64), 2, a_sem.at[m], (q_far, n))

    def b_copy(n):
        return remote(rows(b_send, 64 * n, 64), rows(b_recv, 64 * m, 64), 3, b_sem.at[m], (q_peer, n))

    def vp_copy(b):
        return remote(rows(vf, 64 * b, 32), rows(vf, 64 * b + 32, 32), 4, vp_sem.at[b], (q_peer, m))

    def x_copy(b):
        return remote(rows(yf, 64 * b + 32, 32), rows(yx, 32 * b, 32), 5, x_sem.at[b], (q_peer, m))

    def yf_copy(b):
        return remote(rows(yf, 64 * b, 32), rows(yf_recv, 32 * m, 32), 6, yf_sem.at[m], (q_far, b))

    def yc_copy(b):
        return remote(rows(yc, 64 * b, 64), rows(yc_recv, 64 * m, 64), 7, yc_sem.at[m], (q_peer, b))

    peer_copy = remote(s_one, s_one_peer, 8, peer_sem, (q_peer, m))

    loads[0].wait()
    loads[1].wait()
    pl.semaphore_wait(barrier, 2 * groups)
    peer_copy.start()

    def send_vectors(step, carry):
        p = pair_at(step)
        for n in (2 * p, 2 * p + 1):
            vf_copy(n).start()
            vc_copy(p, n).start()
        return carry

    lax.fori_loop(0, pairs, send_vectors, 0)
    loads[2].wait()
    peer_copy.wait()

    def send_sources(step, carry):
        p = pair_at(step)
        mix_copy(0, p).wait()
        mix_copy(1, p).wait()
        low, high = 2 * p, 2 * p + 1
        first = [rows(s_two, 32 * low, 32)[...], rows(s_two, 32 * high, 32)[...]]
        for k, n in enumerate((low, high)):
            rows(b_send, 64 * n, 32)[...] = dot_nt(first[0], lm[n, k])
            rows(b_send, 64 * n + 32, 32)[...] = dot_nt(first[1], lm[n, 1 - k])
            rows(a_send, 64 * n, 32)[...] = dot_nt(rows(s_one, 32 * n, 32)[...], qm[n, 0])
            rows(a_send, 64 * n + 32, 32)[...] = dot_nt(rows(s_one_peer, 32 * n, 32)[...], qm[n, 1])
        for n in (low, high):
            a_copy(n).start()
            b_copy(n).start()
        return carry

    lax.fori_loop(0, pairs, send_sources, 0)
    loads[3].wait()
    loads[4].wait()
    loads[5].wait()

    def make_targets(step, carry):
        p = pair_at(step)
        mix_copy(2, p).wait()
        mix_copy(3, p).wait()
        low, high = 2 * p, 2 * p + 1
        for basis, mix, out in ((t_one, tm_one, p_one), (t_two, tm_two, p_two)):
            for k, n in enumerate((low, high)):
                t = rows(basis, 32 * n, 32)[...]
                rows(out, 128 * p + 32 * k, 32)[...] = dot(t, mix[n, k])
                rows(out, 128 * p + 64 + 32 * k, 32)[...] = dot(t, mix[n, 1 - k])
        return carry

    lax.fori_loop(0, pairs, make_targets, 0)

    def forward(p):
        for b in (2 * p, 2 * p + 1):
            vf_copy_in = vp_copy(b)
            remote(rows(v_own, 0, 32), rows(vf, 64 * b, 32), 0, vf_sem.at[b], (q_far, m)).wait_recv()
            vf_copy_in.start()

    def apply(p):
        low, high = 2 * p, 2 * p + 1
        for b in (low, high):
            remote(rows(vf, 64 * b, 32), rows(vf, 64 * b + 32, 32), 4, vp_sem.at[b], (q_peer, m)).wait_recv()
            remote(rows(v_own, 0, 64), rows(vc, 64 * b, 64), 1, vc_sem.at[b], (q_peer, m)).wait_recv()
            remote(rows(a_send, 0, 64), rows(a_recv, 64 * b, 64), 2, a_sem.at[b], (q_far, m)).wait_recv()
            remote(rows(b_send, 0, 64), rows(b_recv, 64 * b, 64), 3, b_sem.at[b], (q_peer, m)).wait_recv()
        v = rows(v_own, 64 * p, 64)[...]
        box = rows(near_own, 64 * p, 64)[...]
        w = 0.5 * v + dot(box, v)
        for k, b in enumerate((low, high)):
            f = rows(p_one, 128 * p + 64 * k, 64)[...]
            c = rows(p_two, 128 * p + 64 * k, 64)[...]
            w = w + dot(dot_nt(f, rows(a_recv, 64 * b, 64)[...]), rows(vf, 64 * b, 64)[...])
            w = w + dot(dot_nt(c, rows(b_recv, 64 * b, 64)[...]), rows(vc, 64 * b, 64)[...])
        for k, b in enumerate((low, high)):
            f = rows(p_one, 128 * p + 64 * k, 64)[...]
            c = rows(p_two, 128 * p + 64 * k, 64)[...]
            rows(yf, 64 * b, 64)[...] = dot(dot_nt(rows(a_recv, 64 * b, 64)[...], f), w)
            rows(yc, 64 * b, 64)[...] = dot(dot_nt(rows(b_recv, 64 * b, 64)[...], c), w)
        rows(product, 64 * p, 64)[...] = 0.5 * w + dot_tn(box, w)
        for b in (low, high):
            x_copy(b).start()
            yc_copy(b).start()


    def join(p):
        for b in (2 * p, 2 * p + 1):
            remote(rows(yf, 0, 32), rows(yx, 32 * b, 32), 5, x_sem.at[b], (q_peer, m)).wait_recv()
            rows(yf, 64 * b, 32)[...] += rows(yx, 32 * b, 32)[...]
        for b in (2 * p, 2 * p + 1):
            yf_copy(b).start()

    def stream(step, carry):
        @pl.when(step < pairs)
        def _():
            forward(pair_at(step))

        @pl.when((step >= 1) & (step < pairs + 1))
        def _():
            apply(pair_at(step - 1))

        @pl.when(step >= 2)
        def _():
            join(pair_at(step - 2))

        return carry

    lax.fori_loop(0, pairs + 2, stream, 0)

    def finish(step, carry):
        p = pair_at(step)
        low, high = 2 * p, 2 * p + 1
        for b in (low, high):
            remote(rows(yf, 0, 32), rows(yf_recv, 32 * b, 32), 6, yf_sem.at[b], (q_far, m)).wait_recv()
            remote(rows(yc, 0, 64), rows(yc_recv, 64 * b, 64), 7, yc_sem.at[b], (q_peer, m)).wait_recv()
        here = rows(product, 64 * p, 64)
        here[...] = (
            here[...]
            + rows(yf_recv, 64 * p, 64)[...]
            + (rows(yc_recv, 128 * p, 64)[...] + rows(yc_recv, 128 * p + 64, 64)[...])
        )
        return carry

    lax.fori_loop(0, pairs, finish, 0)

    for k, ref in (
        (0, v_own),
        (1, vc),
        (2, a_send),
        (3, b_send),
        (4, v_own),
        (5, v_own),
        (6, v_own),
        (7, vc),
    ):
        remote(ref, ref, k, peer_sem, (q_peer, m)).wait_send()


def body(sketch, near_field, source_one, source_two, target_one, target_two, quarter_mix, leaf_mix, mix_one, mix_two):
    groups = lax.axis_size("blk")
    local, vectors = sketch.shape
    rank = source_one.shape[1]
    any_space = pl.BlockSpec(memory_space=pl.ANY)
    basis = pltpu.VMEM((local, rank), F32)
    mixes = pltpu.VMEM(quarter_mix.shape, F32)
    single = pltpu.VMEM((local, vectors), F32)
    double = pltpu.VMEM((2 * local, vectors), F32)
    nodes = pltpu.VMEM((2 * local, rank), F32)
    dma = pltpu.SemaphoreType.DMA


    return pl.pallas_call(
        functools.partial(kernel, groups),
        out_shape=jax.ShapeDtypeStruct((local, vectors), F32),
        in_specs=[any_space] * 10,
        out_specs=pl.BlockSpec(memory_space=pltpu.VMEM),
        scratch_shapes=[
            single,
            pltpu.VMEM(near_field.shape, F32),
            basis,
            basis,
            basis,
            basis,
            basis,
            mixes,
            mixes,
            mixes,
            mixes,
            nodes,
            nodes,
            nodes,
            nodes,
            double,
            double,
            nodes,
            nodes,
            double,
            single,
            double,
            single,
            double,
            dma((6,)),
            dma((4, groups // 2)),
            dma(()),
            dma((9,)),
            dma((groups,)),
            dma((groups,)),
            dma((groups,)),
            dma((groups,)),
            dma((groups,)),
            dma((groups,)),
            dma((groups,)),
            dma((groups,)),
        ],
        compiler_params=pltpu.CompilerParams(
            collective_id=0, has_side_effects=True, vmem_limit_bytes=60 * 1024 * 1024
        ),
    )(sketch, near_field, source_one, source_two, target_one, target_two, quarter_mix, leaf_mix, mix_one, mix_two)


def solution(mesh):
    rows_split = P(("half", "blk"), None)
    nodes_split = P(("half", "blk"), None, None, None)
    return jax.shard_map(
        body,
        mesh=mesh,
        in_specs=(rows_split,) * 6 + (nodes_split,) * 4,
        out_specs=rows_split,
        check_vma=False,
    )
```

time: 572 us -> 133 us (0.23)
  the two profiles are of different devices: /device:TPU:1 before, /device:TPU:11 now
where the time goes in v1:
time: 133 us; the launch traced here: 132 us
  Pallas kernels  128 us (96%)
  local copies, waits for them, and re-layouts  4.21 us (3%)
    pallas_call x1, Pallas kernels, body(): pl.pallas_call(functools.partial(kernel, groups), out_shape=jax.ShapeDtyp...  128 us
    unnamed x2, local copies, waits for them, and re-layouts  4.21 us

profile of v1, /device:TPU:11, one launch (start us, length us, event | category | flops | bytes accessed | tf_op | source)
XLA Modules:
  0.0 132.4 jit_solution(12525497004098740604)
XLA Ops:
  0.0 1.9 %copy.11.near = f32[1024,64]{1,0:T(8,128)} copy(f32[1024,64]{0,1:T(8,128)} %param.11) | data formatting | bytes 524288 | tf_op args[1]
  1.9 128.2 %shard_map.100 = f32[1024,256]{1,0:T(8,128)} custom-call(f32[1024,256]{1,0:T(8,128)} %sketch.1, f32[1024,64]{1,0:T(8,128)} %copy.11.near, f32[1024,128]{1,0:T(8,128)} %source_one.1, f32[1024,128]{1,0:T(8,128)} %source_two.1, f32[1024,128]{1,0:T(8,128)} %target_one.1, f32[1024,128]{1,0:T(8,128)} %target_two.1, f32[32,2,128,128]{3,2,1,0:T(8,128)} %quarter_mix.1, ...), custom_call_target="tpu_custom_call" | custom-call | tf_op jit(solution)/shard_map/pallas_call | solution.py:332
  130.1 2.3 %copy.13 = f32[1024,256]{1,0:T(8,128)} copy(f32[1024,256]{1,0:T(8,128)} %shard_map.100) | data formatting | bytes 2097152

commit v2 on v1

--- a/solution.py
+++ b/solution.py
@@ -37,6 +37,11 @@
     for k in range(bits):
         total = total + lax.rem(lax.div(a, 1 << k), 2) * (1 << (bits - 1 - k))
     return total
+
+
+RELAYED = dict(relay=1, cross=2, share=3, target=3, apply=4, join=5, add=6, gather=7)
+STRAIGHT = dict(relay=1, share=1, target=1, apply=2, join=3, gather=4)
+AHEAD = 2
 
 
 def rows(ref, start, count):
@@ -78,6 +83,8 @@
     yf,
     yx,
     yc,
+    yn,
+    yr,
     yf_recv,
     yc_recv,
     load_sem,
@@ -87,22 +94,34 @@
     vf_sem,
     vp_sem,
     vc_sem,
+    vn_sem,
     a_sem,
     b_sem,
     x_sem,
+    yn_sem,
+    yr_sem,
     yf_sem,
     yc_sem,
 ):
     pairs = groups // 2
+    half = pairs // 2
     bits = pairs.bit_length() - 1
     q = lax.axis_index("half")
     m = lax.axis_index("blk")
     mine = lax.div(m, 2)
     q_peer = xor(q, 1, 2)
     q_far = xor(q, 2, 2)
+    beside = xor(m, 1, 1) + 2 * mine
 
     def pair_at(step):
-        return xor(mine, reversed_bits(step, bits), bits)
+        inner = reversed_bits(lax.rem(step, half), bits - 1)
+        return xor(mine, inner + inner - lax.rem(inner, 2) + 2 * lax.div(step, half), bits)
+
+    def direct_at(step):
+        return lax.div(step, half) * 32
+
+    def entry(p):
+        return lax.rem(m + mine + p, 2)
 
     barrier = pltpu.get_barrier_semaphore()
 
@@ -112,6 +131,7 @@
         return carry
 
     lax.fori_loop(0, groups, greet, 0)
+    pl.semaphore_signal(barrier, inc=1, device_id=(q, beside), device_id_type=MESH)
 
     loads = [
         pltpu.make_async_copy(src, dst, load_sem.at[k])
@@ -157,8 +177,15 @@
     def vf_copy(n):
         return remote(rows(v_own, 32 * n, 32), rows(vf, 64 * m, 32), 0, vf_sem.at[m], (q_far, n))
 
-    def vc_copy(p, n):
+    def vc_copy(p):
+        n = 2 * p + entry(p)
         return remote(rows(v_own, 64 * p, 64), rows(vc, 64 * m, 64), 1, vc_sem.at[m], (q_peer, n))
+
+    def vn_copy(b):
+        return remote(rows(vc, 64 * b, 64), rows(vc, 64 * b, 64), 9, vn_sem.at[b], (q, beside))
+
+    def yn_copy(p, b):
+        return remote(rows(yc, 64 * b, 64), rows(yn, 64 * p, 64), 10, yn_sem.at[p], (q, beside))
 
     def a_copy(n):
         return remote(rows(a_send, 64 * n, 64), rows(a_recv, 64 * m, 64), 2, a_sem.at[m], (q_far, n))
@@ -166,152 +193,239 @@
     def b_copy(n):
         return remote(rows(b_send, 64 * n, 64), rows(b_recv, 64 * m, 64), 3, b_sem.at[m], (q_peer, n))
 
-    def vp_copy(b):
-        return remote(rows(vf, 64 * b, 32), rows(vf, 64 * b + 32, 32), 4, vp_sem.at[b], (q_peer, m))
-
-    def x_copy(b):
-        return remote(rows(yf, 64 * b + 32, 32), rows(yx, 32 * b, 32), 5, x_sem.at[b], (q_peer, m))
+    def vr_copy(b):
+        return remote(rows(vc, 64 * b + 32 * lax.rem(m, 2), 32), rows(vf, 64 * b + 32, 32), 11, vf_sem.at[b], (q_far, m))
+
+    def vp_copy(b, off):
+        return remote(rows(vf, 64 * b + 32 - off, 32), rows(vf, 64 * b + off, 32), 4, vp_sem.at[b], (q_peer, m))
+
+    def x_copy(b, off):
+        return remote(rows(yf, 64 * b + off, 32), rows(yx, 32 * b, 32), 5, x_sem.at[b], (q_peer, m))
+
+    def yr_copy(b):
+        return remote(rows(yf, 64 * b + 32, 32), rows(yr, 32 * b, 32), 12, yr_sem.at[b], (q_far, m))
 
     def yf_copy(b):
         return remote(rows(yf, 64 * b, 32), rows(yf_recv, 32 * m, 32), 6, yf_sem.at[m], (q_far, b))
 
     def yc_copy(b):
-        return remote(rows(yc, 64 * b, 64), rows(yc_recv, 64 * m, 64), 7, yc_sem.at[m], (q_peer, b))
+        return remote(rows(yc, 64 * b, 64), rows(yc_recv, 64 * mine, 64), 7, yc_sem.at[mine], (q_peer, b))
 
     peer_copy = remote(s_one, s_one_peer, 8, peer_sem, (q_peer, m))
 
     loads[0].wait()
     loads[1].wait()
-    pl.semaphore_wait(barrier, 2 * groups)
+    pl.semaphore_wait(barrier, 2 * groups + 1)
     peer_copy.start()
 
-    def send_vectors(step, carry):
-        p = pair_at(step)
-        for n in (2 * p, 2 * p + 1):
-            vf_copy(n).start()
-            vc_copy(p, n).start()
-        return carry
-
-    lax.fori_loop(0, pairs, send_vectors, 0)
-    loads[2].wait()
-    peer_copy.wait()
-
-    def send_sources(step, carry):
+    def both(p):
+        return (2 * p, 2 * p + 1)
+
+    def arrived(dst, sem):
+        remote(dst, dst, 0, sem, (q_peer, m)).wait_recv()
+
+    def send_vectors(step):
+        p = pair_at(step)
+        vc_copy(p).start()
+
+        @pl.when(step >= half)
+        def _():
+            for n in both(p):
+                vf_copy(n).start()
+
+    def make_sources(step):
         p = pair_at(step)
         mix_copy(0, p).wait()
         mix_copy(1, p).wait()
-        low, high = 2 * p, 2 * p + 1
-        first = [rows(s_two, 32 * low, 32)[...], rows(s_two, 32 * high, 32)[...]]
-        for k, n in enumerate((low, high)):
+        first = [rows(s_two, 32 * n, 32)[...] for n in both(p)]
+        for k, n in enumerate(both(p)):
             rows(b_send, 64 * n, 32)[...] = dot_nt(first[0], lm[n, k])
             rows(b_send, 64 * n + 32, 32)[...] = dot_nt(first[1], lm[n, 1 - k])
             rows(a_send, 64 * n, 32)[...] = dot_nt(rows(s_one, 32 * n, 32)[...], qm[n, 0])
             rows(a_send, 64 * n + 32, 32)[...] = dot_nt(rows(s_one_peer, 32 * n, 32)[...], qm[n, 1])
-        for n in (low, high):
+
+    def send_sources(step):
+        for n in both(pair_at(step)):
             a_copy(n).start()
             b_copy(n).start()
-        return carry
-
-    lax.fori_loop(0, pairs, send_sources, 0)
-    loads[3].wait()
-    loads[4].wait()
-    loads[5].wait()
-
-    def make_targets(step, carry):
+
+    def make_targets(step):
         p = pair_at(step)
         mix_copy(2, p).wait()
         mix_copy(3, p).wait()
-        low, high = 2 * p, 2 * p + 1
         for basis, mix, out in ((t_one, tm_one, p_one), (t_two, tm_two, p_two)):
-            for k, n in enumerate((low, high)):
+            for k, n in enumerate(both(p)):
                 t = rows(basis, 32 * n, 32)[...]
                 rows(out, 128 * p + 32 * k, 32)[...] = dot(t, mix[n, k])
                 rows(out, 128 * p + 64 + 32 * k, 32)[...] = dot(t, mix[n, 1 - k])
-        return carry
-
-    lax.fori_loop(0, pairs, make_targets, 0)
-
-    def forward(p):
-        for b in (2 * p, 2 * p + 1):
-            vf_copy_in = vp_copy(b)
-            remote(rows(v_own, 0, 32), rows(vf, 64 * b, 32), 0, vf_sem.at[b], (q_far, m)).wait_recv()
-            vf_copy_in.start()
-
-    def apply(p):
-        low, high = 2 * p, 2 * p + 1
-        for b in (low, high):
-            remote(rows(vf, 64 * b, 32), rows(vf, 64 * b + 32, 32), 4, vp_sem.at[b], (q_peer, m)).wait_recv()
-            remote(rows(v_own, 0, 64), rows(vc, 64 * b, 64), 1, vc_sem.at[b], (q_peer, m)).wait_recv()
-            remote(rows(a_send, 0, 64), rows(a_recv, 64 * b, 64), 2, a_sem.at[b], (q_far, m)).wait_recv()
-            remote(rows(b_send, 0, 64), rows(b_recv, 64 * b, 64), 3, b_sem.at[b], (q_peer, m)).wait_recv()
+
+    def relay(step):
+        p = pair_at(step)
+        b = 2 * p + entry(p)
+        arrived(rows(vc, 64 * b, 64), vc_sem.at[b])
+        vn_copy(b).start()
+
+        @pl.when(step < half)
+        def _():
+            vr_copy(b).start()
+
+    def cross(step):
+        p = pair_at(step)
+        b = 2 * p + 1 - entry(p)
+        arrived(rows(vc, 64 * b, 64), vn_sem.at[b])
+        vr_copy(b).start()
+
+    def share(step):
+        off = direct_at(step)
+        for b in both(pair_at(step)):
+            arrived(rows(vf, 64 * b + 32 - off, 32), vf_sem.at[b])
+            vp_copy(b, off).start()
+
+    def apply(step):
+        p = pair_at(step)
+        off = direct_at(step)
+        for b in both(p):
+            arrived(rows(vf, 64 * b + off, 32), vp_sem.at[b])
+            arrived(rows(a_recv, 64 * b, 64), a_sem.at[b])
+            arrived(rows(b_recv, 64 * b, 64), b_sem.at[b])
+        @pl.when(step >= half)
+        def _():
+            b = 2 * p + 1 - entry(p)
+            arrived(rows(vc, 64 * b, 64), vn_sem.at[b])
+
         v = rows(v_own, 64 * p, 64)[...]
         box = rows(near_own, 64 * p, 64)[...]
         w = 0.5 * v + dot(box, v)
-        for k, b in enumerate((low, high)):
+        for k, b in enumerate(both(p)):
             f = rows(p_one, 128 * p + 64 * k, 64)[...]
             c = rows(p_two, 128 * p + 64 * k, 64)[...]
             w = w + dot(dot_nt(f, rows(a_recv, 64 * b, 64)[...]), rows(vf, 64 * b, 64)[...])
             w = w + dot(dot_nt(c, rows(b_recv, 64 * b, 64)[...]), rows(vc, 64 * b, 64)[...])
-        for k, b in enumerate((low, high)):
+        for k, b in enumerate(both(p)):
             f = rows(p_one, 128 * p + 64 * k, 64)[...]
             c = rows(p_two, 128 * p + 64 * k, 64)[...]
             rows(yf, 64 * b, 64)[...] = dot(dot_nt(rows(a_recv, 64 * b, 64)[...], f), w)
             rows(yc, 64 * b, 64)[...] = dot(dot_nt(rows(b_recv, 64 * b, 64)[...], c), w)
         rows(product, 64 * p, 64)[...] = 0.5 * w + dot_tn(box, w)
-        for b in (low, high):
-            x_copy(b).start()
-            yc_copy(b).start()
-
-
-    def join(p):
-        for b in (2 * p, 2 * p + 1):
-            remote(rows(yf, 0, 32), rows(yx, 32 * b, 32), 5, x_sem.at[b], (q_peer, m)).wait_recv()
-            rows(yf, 64 * b, 32)[...] += rows(yx, 32 * b, 32)[...]
-        for b in (2 * p, 2 * p + 1):
-            yf_copy(b).start()
+
+    def send_applied(step):
+        p = pair_at(step)
+        off = direct_at(step)
+        for b in both(p):
+            x_copy(b, off).start()
+
+        @pl.when(step >= half)
+        def _():
+            yn_copy(p, 2 * p + 1 - entry(p)).start()
+
+    def join(step):
+        off = direct_at(step)
+        for b in both(pair_at(step)):
+            arrived(rows(yx, 32 * b, 32), x_sem.at[b])
+            rows(yf, 64 * b + 32 - off, 32)[...] += rows(yx, 32 * b, 32)[...]
+
+    def send_joined(step):
+        p = pair_at(step)
+
+        @pl.when(step < half)
+        def _():
+            for b in both(p):
+                yr_copy(b).start()
+
+        @pl.when(step >= half)
+        def _():
+            for b in both(p):
+                yf_copy(b).start()
+
+    def add(step):
+        for b in both(pair_at(step)):
+            arrived(rows(yr, 32 * b, 32), yr_sem.at[b])
+            rows(yc, 64 * b + 32 * lax.rem(m, 2), 32)[...] += rows(yr, 32 * b, 32)[...]
+
+    def send_added(step):
+        p = pair_at(step)
+        yn_copy(p, 2 * p + 1 - entry(p)).start()
+
+    def gather(step):
+        p = pair_at(step)
+        b = 2 * p + entry(p)
+        arrived(rows(yn, 64 * p, 64), yn_sem.at[p])
+        rows(yc, 64 * b, 64)[...] += rows(yn, 64 * p, 64)[...]
+
+    def send_gathered(step):
+        p = pair_at(step)
+        yc_copy(2 * p + entry(p)).start()
+
+    def staged(step, stage, lag, first, last):
+        @pl.when((step >= first + lag) & (step < last + lag))
+        def _():
+            stage(step - lag)
+
+    def staggered(step, name, *stages):
+        for stage in stages:
+            if name in RELAYED:
+                staged(step, stage, RELAYED[name], 0, half)
+            if name in STRAIGHT:
+                staged(step, stage, STRAIGHT[name], half, pairs)
+
+    for step in range(AHEAD):
+        send_vectors(step)
+    for copy in loads[2:]:
+        copy.wait()
+    peer_copy.wait()
 
     def stream(step, carry):
-        @pl.when(step < pairs)
-        def _():
-            forward(pair_at(step))
-
-        @pl.when((step >= 1) & (step < pairs + 1))
-        def _():
-            apply(pair_at(step - 1))
-
-        @pl.when(step >= 2)
-        def _():
-            join(pair_at(step - 2))
-
+        @pl.when(step < pairs - AHEAD)
+        def _():
+            send_vectors(step + AHEAD)
+
+        staged(step, make_sources, 0, 0, pairs)
+        staggered(step, "relay", relay)
+        staggered(step, "cross", cross)
+        staggered(step, "share", share)
+        staged(step, send_sources, 0, 0, pairs)
+        staggered(step, "gather", gather)
+        staggered(step, "add", add)
+        staggered(step, "join", join)
+        staggered(step, "gather", send_gathered)
+        staggered(step, "add", send_added)
+        staggered(step, "join", send_joined)
+        staggered(step, "target", make_targets)
+        staggered(step, "apply", apply)
+        staggered(step, "apply", send_applied)
         return carry
 
-    lax.fori_loop(0, pairs + 2, stream, 0)
+    lax.fori_loop(0, half + max(RELAYED["gather"], half + STRAIGHT["gather"]), stream, 0)
 
     def finish(step, carry):
         p = pair_at(step)
-        low, high = 2 * p, 2 * p + 1
-        for b in (low, high):
-            remote(rows(yf, 0, 32), rows(yf_recv, 32 * b, 32), 6, yf_sem.at[b], (q_far, m)).wait_recv()
-            remote(rows(yc, 0, 64), rows(yc_recv, 64 * b, 64), 7, yc_sem.at[b], (q_peer, m)).wait_recv()
-        here = rows(product, 64 * p, 64)
-        here[...] = (
-            here[...]
-            + rows(yf_recv, 64 * p, 64)[...]
-            + (rows(yc_recv, 128 * p, 64)[...] + rows(yc_recv, 128 * p + 64, 64)[...])
-        )
+        arrived(rows(yc_recv, 64 * p, 64), yc_sem.at[p])
+        rows(product, 64 * p, 64)[...] += rows(yc_recv, 64 * p, 64)[...]
+
+        @pl.when(step >= half)
+        def _():
+            for b in both(p):
+                arrived(rows(yf_recv, 32 * b, 32), yf_sem.at[b])
+            rows(product, 64 * p, 64)[...] += rows(yf_recv, 64 * p, 64)[...]
+
         return carry
 
     lax.fori_loop(0, pairs, finish, 0)
 
+    whole, part = v_own, rows(v_own, 0, 16 * groups)
     for k, ref in (
-        (0, v_own),
-        (1, vc),
+        (0, part),
+        (1, whole),
         (2, a_send),
         (3, b_send),
-        (4, v_own),
-        (5, v_own),
-        (6, v_own),
-        (7, vc),
+        (4, whole),
+        (5, whole),
+        (6, part),
+        (7, whole),
+        (9, whole),
+        (10, whole),
+        (11, part),
+        (12, part),
     ):
         remote(ref, ref, k, peer_sem, (q_peer, m)).wait_send()
 
@@ -358,19 +472,24 @@
             single,
             double,
             single,
-            double,
+            single,
+            single,
+            single,
             dma((6,)),
             dma((4, groups // 2)),
             dma(()),
-            dma((9,)),
-            dma((groups,)),
-            dma((groups,)),
-            dma((groups,)),
-            dma((groups,)),
-            dma((groups,)),
-            dma((groups,)),
-            dma((groups,)),
-            dma((groups,)),
+            dma((13,)),
+            dma((groups,)),
+            dma((groups,)),
+            dma((groups,)),
+            dma((groups,)),
+            dma((groups,)),
+            dma((groups,)),
+            dma((groups,)),
+            dma((groups // 2,)),
+            dma((groups,)),
+            dma((groups,)),
+            dma((groups // 2,)),
         ],
         compiler_params=pltpu.CompilerParams(
             collective_id=0, has_side_effects=True, vmem_limit_bytes=60 * 1024 * 1024

time: 133 us -> 116 us (0.87)
  the two profiles are of different devices: /device:TPU:11 before, /device:TPU:1 now
where the time goes in v2:
time: 116 us; the launch traced here: 115 us
  Pallas kernels  111 us (96%)
  local copies, waits for them, and re-layouts  4.21 us (4%)
    pallas_call x1, Pallas kernels, body(): pl.pallas_call(functools.partial(kernel, groups), out_shape=jax.ShapeDtyp...  111 us
    unnamed x2, local copies, waits for them, and re-layouts  4.21 us

profile of v2, /device:TPU:1, one launch (start us, length us, event | category | flops | bytes accessed | tf_op | source)
XLA Modules:
  0.0 115.4 jit_solution(16693925292931517267)
XLA Ops:
  0.0 1.9 %copy.11.near = f32[1024,64]{1,0:T(8,128)} copy(f32[1024,64]{0,1:T(8,128)} %param.11) | data formatting | bytes 524288 | tf_op args[1]
  1.9 111.2 %shard_map.100 = f32[1024,256]{1,0:T(8,128)} custom-call(f32[1024,256]{1,0:T(8,128)} %sketch.1, f32[1024,64]{1,0:T(8,128)} %copy.11.near, f32[1024,128]{1,0:T(8,128)} %source_one.1, f32[1024,128]{1,0:T(8,128)} %source_two.1, f32[1024,128]{1,0:T(8,128)} %target_one.1, f32[1024,128]{1,0:T(8,128)} %target_two.1, f32[32,2,128,128]{3,2,1,0:T(8,128)} %quarter_mix.1, ...), custom_call_target="tpu_custom_call" | custom-call | tf_op jit(solution)/shard_map/pallas_call | solution.py:446
  113.1 2.3 %copy.13 = f32[1024,256]{1,0:T(8,128)} copy(f32[1024,256]{1,0:T(8,128)} %shard_map.100) | data formatting | bytes 2097152

commit v3 on v2

--- a/solution.py
+++ b/solution.py
@@ -62,6 +62,7 @@
     target_mix_two,
     product,
     v_own,
+    near_flat,
     near_own,
     s_one,
     s_one_peer,
@@ -115,6 +116,7 @@
 
     def pair_at(step):
         inner = reversed_bits(lax.rem(step, half), bits - 1)
+        inner = inner + lax.div(step, half) * (half - 1 - 2 * inner)
         return xor(mine, inner + inner - lax.rem(inner, 2) + 2 * lax.div(step, half), bits)
 
     def direct_at(step):
@@ -142,7 +144,7 @@
                 (source_two, s_two),
                 (target_one, t_one),
                 (target_two, t_two),
-                (near, near_own),
+                (near, near_flat),
             )
         )
     ]
@@ -372,6 +374,8 @@
         send_vectors(step)
     for copy in loads[2:]:
         copy.wait()
+    for k in range(near_own.shape[0] // 128):
+        near_own[pl.ds(128 * k, 128)] = near_flat[:, pl.ds(128 * k, 128)].T
     peer_copy.wait()
 
     def stream(step, carry):
@@ -450,6 +454,7 @@
         out_specs=pl.BlockSpec(memory_space=pltpu.VMEM),
         scratch_shapes=[
             single,
+            pltpu.VMEM(near_field.shape[::-1], F32),
             pltpu.VMEM(near_field.shape, F32),
             basis,
             basis,
@@ -494,7 +499,7 @@
         compiler_params=pltpu.CompilerParams(
             collective_id=0, has_side_effects=True, vmem_limit_bytes=60 * 1024 * 1024
         ),
-    )(sketch, near_field, source_one, source_two, target_one, target_two, quarter_mix, leaf_mix, mix_one, mix_two)
+    )(sketch, near_field.T, source_one, source_two, target_one, target_two, quarter_mix, leaf_mix, mix_one, mix_two)
 
 
 def solution(mesh):

time: 116 us -> 114 us (0.983)
  local copies, waits for them, and re-layouts: 4.21 us -> 2.26 us
    unnamed x2 -> x1, local copies, waits for them, and re-layouts: 4.21 us -> 2.26 us
where the time goes in v3:
time: 114 us
  Pallas kernels  111 us (97%)
  local copies, waits for them, and re-layouts  2.26 us (2%)
    pallas_call x1, Pallas kernels, body(): pl.pallas_call(functools.partial(kernel, groups), out_shape=jax.ShapeDtyp...  111 us

profile of v3, /device:TPU:1, one launch (start us, length us, event | category | flops | bytes accessed | tf_op | source)
XLA Modules:
  0.0 113.7 jit_solution(7676915206907616840)
XLA Ops:
  0.0 111.4 %shard_map.100 = f32[1024,256]{1,0:T(8,128)} custom-call(f32[1024,256]{1,0:T(8,128)} %sketch.1, f32[64,1024]{1,0:T(8,128)} %bitcast.1, f32[1024,128]{1,0:T(8,128)} %source_one.1, f32[1024,128]{1,0:T(8,128)} %source_two.1, f32[1024,128]{1,0:T(8,128)} %target_one.1, f32[1024,128]{1,0:T(8,128)} %target_two.1, f32[32,2,128,128]{3,2,1,0:T(8,128)} %quarter_mix.1, ...), custom_call_target="tpu_custom_call" | custom-call | tf_op jit(solution)/shard_map/pallas_call | solution.py:450
  111.4 2.3 %copy.12 = f32[1024,256]{1,0:T(8,128)} copy(f32[1024,256]{1,0:T(8,128)} %shard_map.100) | data formatting | bytes 2097152

commit v4 on v3

--- a/solution.py
+++ b/solution.py
@@ -383,10 +383,10 @@
         def _():
             send_vectors(step + AHEAD)
 
-        staged(step, make_sources, 0, 0, pairs)
         staggered(step, "relay", relay)
         staggered(step, "cross", cross)
         staggered(step, "share", share)
+        staged(step, make_sources, 0, 0, pairs)
         staged(step, send_sources, 0, 0, pairs)
         staggered(step, "gather", gather)
         staggered(step, "add", add)

time: 114 us -> 111 us (0.974)
  Pallas kernels: 111 us -> 109 us
    pallas_call x1, Pallas kernels: 111 us -> 109 us  [body(): pl.pallas_call(functools.partial(kernel, groups), out_shape=jax.ShapeDtyp...]
where the time goes in v4:
time: 111 us
  Pallas kernels  109 us (98%)
  local copies, waits for them, and re-layouts  2.26 us (2%)
    pallas_call x1, Pallas kernels, body(): pl.pallas_call(functools.partial(kernel, groups), out_shape=jax.ShapeDtyp...  109 us
    unnamed x1, local copies, waits for them, and re-layouts  2.26 us

profile of v4, /device:TPU:1, one launch (start us, length us, event | category | flops | bytes accessed | tf_op | source)
XLA Modules:
  0.0 111.1 jit_solution(4894522018967979519)
XLA Ops:
  0.0 108.8 %shard_map.100 = f32[1024,256]{1,0:T(8,128)} custom-call(f32[1024,256]{1,0:T(8,128)} %sketch.1, f32[64,1024]{1,0:T(8,128)} %bitcast.1, f32[1024,128]{1,0:T(8,128)} %source_one.1, f32[1024,128]{1,0:T(8,128)} %source_two.1, f32[1024,128]{1,0:T(8,128)} %target_one.1, f32[1024,128]{1,0:T(8,128)} %target_two.1, f32[32,2,128,128]{3,2,1,0:T(8,128)} %quarter_mix.1, ...), custom_call_target="tpu_custom_call" | custom-call | tf_op jit(solution)/shard_map/pallas_call | solution.py:450
  108.9 2.3 %copy.12 = f32[1024,256]{1,0:T(8,128)} copy(f32[1024,256]{1,0:T(8,128)} %shard_map.100) | data formatting | bytes 2097152
